TPU v7x, 32 devices: a whole 2x2x4 slice. The times are simulated.
32 devices in a mesh: batch: 2 (over x), row: 4 (over z), col: 4 (over y, core).
Axes of the slice: x: 2, y: 2, z: 4, core: 2. Of those that a mesh axis runs over, the one named last changes fastest.
Arguments:
- spd_blocks: float32 [64, 256, 8192], P(('batch', 'row'), None, 'col'), parts along dimension 0
Outputs:
- output: float32 [64, 256, 8192], P(('batch', 'row'), None, 'col'), parts along dimension 0
There are 2 independent parts. A program takes and returns all parts, laid end to end along the dimension named above; each array names one.
All inputs are finite; a program needn't handle non-finite values.
Results may differ from a plain program's by a relative error of at most 0.001.
Values are sent between devices in bfloat16 or wider.
A program may use at most 1 GiB of HBM per device.

v0:
```python
import functools
import jax
import jax.numpy as jnp
from jax import lax
from jax.sharding import PartitionSpec as P, NamedSharding


def transposed_panel(row_panel, row_id, col_id, row_devs, col_devs, row_skip, col_skip):
    row_blocks = row_panel.shape[0]
    blk_size = row_panel.shape[1]
    if row_devs >= col_devs:
        grid_ratio = row_devs // col_devs
        blk_shift = (row_skip * row_devs - col_skip * col_devs) // col_devs
        pick_mask = (jnp.arange(grid_ratio) == row_id // col_devs) & (row_id % col_devs == col_id)
        spread = (row_panel[:, None] * pick_mask.astype(jnp.bfloat16)[None, :, None, None]).reshape(row_blocks * grid_ratio, blk_size, blk_size)
        if blk_shift >= 0:
            spread = jnp.pad(spread, ((blk_shift, 0), (0, 0), (0, 0)))
        else:
            spread = spread[-blk_shift:]
    else:
        grid_ratio = col_devs // row_devs
        blk_shift = (col_skip * col_devs - row_skip * row_devs) // row_devs
        if blk_shift >= 0:
            shifted = row_panel[blk_shift:]
        else:
            shifted = jnp.pad(row_panel, ((-blk_shift, 0), (0, 0), (0, 0)))
        grouped = shifted.reshape(shifted.shape[0] // grid_ratio, grid_ratio, blk_size, blk_size)
        chosen = lax.dynamic_index_in_dim(grouped, col_id // row_devs, axis=1, keepdims=False)
        spread = jnp.where(row_id == col_id % row_devs, chosen, jnp.zeros_like(chosen))
    return lax.psum(spread, "row")


def solution(mesh):
    row_devs = mesh.shape["row"]
    col_devs = mesh.shape["col"]

    def factor_local(a_loc):
        row_blocks, blk_size, local_cols = a_loc.shape
        col_blocks = local_cols // blk_size
        blk_count = row_blocks * row_devs
        row_id = lax.axis_index("row")
        col_id = lax.axis_index("col")
        eye_blk = jnp.eye(blk_size, dtype=jnp.float32)

        def panel_step(step_idx, window):
            win_rows, win_cols = window.shape
            win_rblk = win_rows // blk_size
            row_skip = row_blocks - win_rblk
            col_skip = col_blocks - win_cols // blk_size
            own_col = col_id == step_idx % col_devs
            is_owner = own_col & (row_id == step_idx % row_devs)
            col_off = (step_idx // col_devs - col_skip) * blk_size
            col_blk = lax.dynamic_slice_in_dim(window, col_off, blk_size, axis=1)
            diag_blk = lax.dynamic_slice_in_dim(col_blk, (step_idx // row_devs - row_skip) * blk_size, blk_size, axis=0)
            diag_own = jnp.tril(jnp.linalg.cholesky(jnp.where(is_owner, diag_blk, eye_blk)))
            diag_fac = lax.psum(jnp.where(is_owner, diag_own, 0.0), "row")
            diag_fac = jnp.where(own_col, diag_fac, eye_blk)
            solved = lax.linalg.triangular_solve(diag_fac, col_blk, left_side=False, lower=True, transpose_a=True)
            row_ids = (row_skip + jnp.arange(win_rblk)) * row_devs + row_id
            below_mask = (row_ids > step_idx)[:, None, None]
            on_diag = (row_ids == step_idx)[:, None, None]
            solved_blocks = solved.reshape(win_rblk, blk_size, blk_size)
            prior_col = col_blk.reshape(win_rblk, blk_size, blk_size)
            new_col = jnp.where(below_mask, solved_blocks, jnp.where(on_diag, diag_fac[None], prior_col))
            new_col = jnp.where(own_col, new_col, prior_col).reshape(win_rows, blk_size)
            window = lax.dynamic_update_slice_in_dim(window, new_col, col_off, axis=1)
            row_panel = lax.psum(jnp.where(below_mask & own_col, solved_blocks, 0.0).astype(jnp.bfloat16), "col")
            col_panel = transposed_panel(row_panel, row_id, col_id, row_devs, col_devs, row_skip, col_skip)
            update = lax.dot_general(row_panel.reshape(win_rows, blk_size), col_panel.reshape(win_cols, blk_size), (((1,), (1,)), ((), ())), preferred_element_type=jnp.float32)
            return window - update

        work_mat = a_loc.reshape(row_blocks * blk_size, local_cols)
        phase_count = min(blk_count, 8)
        bounds = [(phase_idx * blk_count) // phase_count for phase_idx in range(phase_count + 1)]
        for phase_idx in range(phase_count):
            row_start = (bounds[phase_idx] // row_devs) * blk_size
            col_start = (bounds[phase_idx] // col_devs) * blk_size
            window = lax.fori_loop(bounds[phase_idx], bounds[phase_idx + 1], panel_step, work_mat[row_start:, col_start:])
            work_mat = lax.dynamic_update_slice(work_mat, window, (row_start, col_start))
        row_blk_ids = jnp.arange(row_blocks) * row_devs + row_id
        col_blk_ids = jnp.arange(col_blocks) * col_devs + col_id
        keep_mask = row_blk_ids[:, None, None, None] >= col_blk_ids[None, None, :, None]
        factor = jnp.where(keep_mask, work_mat.reshape(row_blocks, blk_size, col_blocks, blk_size), 0.0)
        return factor.reshape(row_blocks, blk_size, local_cols)

    blk_spec = P(("batch", "row"), None, "col")
    return jax.shard_map(factor_local, mesh=mesh, in_specs=(blk_spec,), out_specs=blk_spec, check_vma=False)
```

profile of v0, /device:TPU:31, one launch (start us, length us, event | category | flops | bytes accessed | tf_op | source)
XLA Modules:
  0.0 6422.7 jit_solution(1258366377272137320)
XLA Ops:
  24.9 931.9 %while.185 = (s32[]{:T(128)}, f32[2048,2048]{0,1:T(8,128)}, s32[]{:T(128)}, s32[]{:T(128)}, pred[1]{0:T(512)(128)(4,1)}, /*index=5*/s32[]{:T(128)}, s32[]{:T(128...) while((s32[]{:T(128)}, f32[2048,2048]{0,1:T(8,128)}, ...), condition=%wide.region_8.10_spmd.clone.clone, body=%wide.region_0.9_spmd.clone.clone.sunk | while | flops 3417915648 | bytes 170937136 | solution.py:78
  129.4 38.5 all-reduce.28.cloned.1.call-done
  358.5 38.5 all-reduce.28.cloned.1.call-done
  587.6 39.4 all-reduce.28.cloned.1.call-done
  818.6 37.5 all-reduce.28.cloned.1.call-done
  967.0 891.6 %while.187 = (s32[]{:T(128)}, f32[1792,1792]{0,1:T(8,128)}, s32[]{:T(128)}, s32[]{:T(128)}, pred[1]{0:T(512)(128)(4,1)}, /*index=5*/s32[]{:T(128)}, s32[]{:T(128...) while((s32[]{:T(128)}, f32[1792,1792]{0,1:T(8,128)}, ...), condition=%wide.region_13.15_spmd.clone.clone, body=%wide.region_9.14_spmd.clone.clone.sunk | while | flops 2761802240 | bytes 136332176 | solution.py:78
  1123.5 36.8 all-reduce.36.cloned.1.call-done
  1342.5 36.8 all-reduce.36.cloned.1.call-done
  1562.3 36.9 all-reduce.36.cloned.1.call-done
  1781.3 36.8 all-reduce.36.cloned.1.call-done
  1877.1 836.6 %while.189 = (s32[]{:T(128)}, f32[1536,1536]{0,1:T(8,128)}, s32[]{:T(128)}, s32[]{:T(128)}, pred[1]{0:T(512)(128)(4,1)}, /*index=5*/s32[]{:T(128)}, s32[]{:T(128...) while((s32[]{:T(128)}, f32[1536,1536]{0,1:T(8,128)}, ...), condition=%wide.region_18.20_spmd.clone.clone, body=%wide.region_14.19_spmd.clone.clone.sunk | while | flops 2172928512 | bytes 109591456 | solution.py:78
  2025.9 37.9 all-reduce.42.cloned.1.call-done
  2231.4 37.9 all-reduce.42.cloned.1.call-done
  2437.8 37.9 all-reduce.42.cloned.1.call-done
  2643.3 37.9 all-reduce.42.cloned.1.call-done
  2725.6 798.0 %while.191 = (s32[]{:T(128)}, f32[1280,1280]{0,1:T(8,128)}, s32[]{:T(128)}, s32[]{:T(128)}, pred[1]{0:T(512)(128)(4,1)}, /*index=5*/s32[]{:T(128)}, s32[]{:T(128...) while((s32[]{:T(128)}, f32[1280,1280]{0,1:T(8,128)}, ...), condition=%wide.region_23.25_spmd.clone.clone, body=%wide.region_19.24_spmd.clone.clone.sunk | while | flops 1651294464 | bytes 83899272 | solution.py:78
  2869.3 36.3 all-reduce.48.cloned.1.call-done
  3065.5 36.5 all-reduce.48.cloned.1.call-done
  3262.8 36.3 all-reduce.48.cloned.1.call-done
  3459.1 36.3 all-reduce.48.cloned.1.call-done
  3532.4 768.5 %while.193 = (s32[]{:T(128)}, f32[1024,1024]{0,1:T(8,128)}, s32[]{:T(128)}, s32[]{:T(128)}, pred[1]{0:T(512)(128)(4,1)}, /*index=5*/s32[]{:T(128)}, s32[]{:T(128...) while((s32[]{:T(128)}, f32[1024,1024]{0,1:T(8,128)}, ...), condition=%wide.region_28.30_spmd.clone.clone, body=%wide.region_24.29_spmd.clone.clone.sunk | while | flops 1196900608 | bytes 63974280 | solution.py:78
  4306.0 719.6 %while.195 = (s32[]{:T(128)}, f32[768,768]{0,1:T(8,128)S(1)}, s32[]{:T(128)}, s32[]{:T(128)}, pred[1]{0:T(512)(128)(4,1)}, /*index=5*/s32[]{:T(128)}, s32[]{:T(1...) while((s32[]{:T(128)}, f32[768,768]{0,1:T(8,128)S(1)}, ...), condition=%wide.region_33.35_spmd.clone.clone, body=%wide.region_29.34_spmd.clone.clone.sunk | while | flops 809746752 | bytes 45097888 | solution.py:78
  5027.4 684.1 %while.197 = (s32[]{:T(128)}, f32[512,512]{0,1:T(8,128)S(1)}, s32[]{:T(128)}, s32[]{:T(128)}, pred[1]{0:T(512)(128)(4,1)}, /*index=5*/s32[]{:T(128)}, s32[]{:T(1...) while((s32[]{:T(128)}, f32[512,512]{0,1:T(8,128)S(1)}, ...), condition=%wide.region_38.40_spmd.clone.clone, body=%wide.region_34.39_spmd.clone.clone.sunk | while | flops 489832768 | bytes 29367156 | solution.py:78
  5712.5 672.7 %while.199 = (s32[]{:T(128)}, f32[256,256]{0,1:T(8,128)S(1)}, s32[]{:T(128)}, s32[1]{0:T(128)}, s32[]{:T(128)}, /*index=5*/pred[1]{0:T(512)(128)(4,1)}, s32[]{:T...) while((s32[]{:T(128)}, f32[256,256]{0,1:T(8,128)S(1)}, ...), condition=%wide.region_43.45_spmd.clone.clone, body=%wide.region_39.44_spmd.clone.clone.sunk | while | flops 237355280 | bytes 12323468 | solution.py:78
  (2152 shorter events, 5827.4 us)
Async XLA Ops:
  64.2 103.7 %all-reduce.28.cloned.1.call-start = ((), (), s32[]{:S(2)}) async-start(), calls=%async_computation.1 | async-start | bytes 2097152 | tf_op jit(solution)/shard_map/while/body/eval_jaxpr/psum | solution.py:67
  293.5 103.6 %all-reduce.28.cloned.1.call-start = ((), (), s32[]{:S(2)}) async-start(), calls=%async_computation.1 | async-start | bytes 2097152 | tf_op jit(solution)/shard_map/while/body/eval_jaxpr/psum | solution.py:67
  522.6 104.5 %all-reduce.28.cloned.1.call-start = ((), (), s32[]{:S(2)}) async-start(), calls=%async_computation.1 | async-start | bytes 2097152 | tf_op jit(solution)/shard_map/while/body/eval_jaxpr/psum | solution.py:67
  752.6 103.6 %all-reduce.28.cloned.1.call-start = ((), (), s32[]{:S(2)}) async-start(), calls=%async_computation.1 | async-start | bytes 2097152 | tf_op jit(solution)/shard_map/while/body/eval_jaxpr/psum | solution.py:67
  1006.4 103.6 %all-reduce.34.cloned.1.call-start = ((), (), s32[]{:S(2)}) async-start(), calls=%async_computation.4 | async-start | bytes 1835008 | tf_op jit(solution)/shard_map/while/body/eval_jaxpr/psum | solution.py:67
  1225.3 103.7 %all-reduce.34.cloned.1.call-start = ((), (), s32[]{:S(2)}) async-start(), calls=%async_computation.4 | async-start | bytes 1835008 | tf_op jit(solution)/shard_map/while/body/eval_jaxpr/psum | solution.py:67
  1444.3 104.6 %all-reduce.34.cloned.1.call-start = ((), (), s32[]{:S(2)}) async-start(), calls=%async_computation.4 | async-start | bytes 1835008 | tf_op jit(solution)/shard_map/while/body/eval_jaxpr/psum | solution.py:67
  1664.1 103.7 %all-reduce.34.cloned.1.call-start = ((), (), s32[]{:S(2)}) async-start(), calls=%async_computation.4 | async-start | bytes 1835008 | tf_op jit(solution)/shard_map/while/body/eval_jaxpr/psum | solution.py:67
  1916.5 100.5 %all-reduce.40.cloned.1.call-start = ((), (), s32[]{:S(2)}) async-start(), calls=%async_computation.7 | async-start | bytes 1572864 | tf_op jit(solution)/shard_map/while/body/eval_jaxpr/psum | solution.py:67
  2121.9 100.5 %all-reduce.40.cloned.1.call-start = ((), (), s32[]{:S(2)}) async-start(), calls=%async_computation.7 | async-start | bytes 1572864 | tf_op jit(solution)/shard_map/while/body/eval_jaxpr/psum | solution.py:67
  2327.4 101.5 %all-reduce.40.cloned.1.call-start = ((), (), s32[]{:S(2)}) async-start(), calls=%async_computation.7 | async-start | bytes 1572864 | tf_op jit(solution)/shard_map/while/body/eval_jaxpr/psum | solution.py:67
  2533.8 100.5 %all-reduce.40.cloned.1.call-start = ((), (), s32[]{:S(2)}) async-start(), calls=%async_computation.7 | async-start | bytes 1572864 | tf_op jit(solution)/shard_map/while/body/eval_jaxpr/psum | solution.py:67
  2764.9 98.7 %all-reduce.46.cloned.1.call-start = ((), (), s32[]{:S(2)}) async-start(), calls=%async_computation.10 | async-start | bytes 1310720 | tf_op jit(solution)/shard_map/while/body/eval_jaxpr/psum | solution.py:67
  2960.0 99.8 %all-reduce.46.cloned.1.call-start = ((), (), s32[]{:S(2)}) async-start(), calls=%async_computation.10 | async-start | bytes 1310720 | tf_op jit(solution)/shard_map/while/body/eval_jaxpr/psum | solution.py:67
  3156.3 100.8 %all-reduce.46.cloned.1.call-start = ((), (), s32[]{:S(2)}) async-start(), calls=%async_computation.10 | async-start | bytes 1310720 | tf_op jit(solution)/shard_map/while/body/eval_jaxpr/psum | solution.py:67
  3353.5 99.9 %all-reduce.46.cloned.1.call-start = ((), (), s32[]{:S(2)}) async-start(), calls=%async_computation.10 | async-start | bytes 1310720 | tf_op jit(solution)/shard_map/while/body/eval_jaxpr/psum | solution.py:67
  3571.7 98.9 %all-reduce.52.cloned.1.call-start = ((), (), s32[]{:S(2)}) async-start(), calls=%async_computation.13 | async-start | bytes 1048576 | tf_op jit(solution)/shard_map/while/body/eval_jaxpr/psum | solution.py:67
  3760.5 98.9 %all-reduce.52.cloned.1.call-start = ((), (), s32[]{:S(2)}) async-start(), calls=%async_computation.13 | async-start | bytes 1048576 | tf_op jit(solution)/shard_map/while/body/eval_jaxpr/psum | solution.py:67
  3949.4 99.9 %all-reduce.52.cloned.1.call-start = ((), (), s32[]{:S(2)}) async-start(), calls=%async_computation.13 | async-start | bytes 1048576 | tf_op jit(solution)/shard_map/while/body/eval_jaxpr/psum | solution.py:67
  4139.3 98.9 %all-reduce.52.cloned.1.call-start = ((), (), s32[]{:S(2)}) async-start(), calls=%async_computation.13 | async-start | bytes 1048576 | tf_op jit(solution)/shard_map/while/body/eval_jaxpr/psum | solution.py:67
  4343.5 97.9 %all-reduce.58.cloned.1.call-start = ((), (), s32[]{:S(2)}) async-start(), calls=%async_computation.16 | async-start | bytes 786432 | tf_op jit(solution)/shard_map/while/body/eval_jaxpr/psum | solution.py:67
  4522.5 98.6 %all-reduce.58.cloned.1.call-start = ((), (), s32[]{:S(2)}) async-start(), calls=%async_computation.16 | async-start | bytes 786432 | tf_op jit(solution)/shard_map/while/body/eval_jaxpr/psum | solution.py:67
  4702.2 99.5 %all-reduce.58.cloned.1.call-start = ((), (), s32[]{:S(2)}) async-start(), calls=%async_computation.16 | async-start | bytes 786432 | tf_op jit(solution)/shard_map/while/body/eval_jaxpr/psum | solution.py:67
  4883.0 98.6 %all-reduce.58.cloned.1.call-start = ((), (), s32[]{:S(2)}) async-start(), calls=%async_computation.16 | async-start | bytes 786432 | tf_op jit(solution)/shard_map/while/body/eval_jaxpr/psum | solution.py:67
  (116 other events, 6744.7 us)
Sparse Core Ops, SparseCore 0:
  129.5 38.4 all-reduce.27
  170.7 51.5 all-reduce.29
  358.6 38.4 all-reduce.27
  399.8 51.5 all-reduce.29
  587.7 39.3 all-reduce.27
  629.8 51.5 all-reduce.29
  858.9 51.5 all-reduce.29
  1112.4 47.9 all-reduce.35
  1331.3 47.9 all-reduce.35
  1511.0 37.8 all-reduce.33
  1551.2 47.9 all-reduce.35
  1770.2 47.9 all-reduce.35
  2019.2 44.5 all-reduce.41
  2224.7 44.5 all-reduce.41
  2431.1 44.5 all-reduce.41
  2636.6 44.5 all-reduce.41
  2865.8 39.7 all-reduce.47
  3062.2 39.7 all-reduce.47
  3259.4 39.7 all-reduce.47
  3455.6 39.7 all-reduce.47
  3672.8 37.8 all-reduce.53
  3861.7 37.8 all-reduce.53
  4051.6 37.8 all-reduce.53
  4240.6 37.8 all-reduce.53
  (72 shorter events, 2469.6 us)
where the time goes:
time: 6460 us; the launch traced here: 6420 us
  waiting for transfers between devices  3100 us (48%)
  other arithmetic  1980 us (31%)
  local copies, waits for them, and re-layouts  867 us (13%)
  matrix products  338 us (5%)
  loops' own time  120 us (2%)
    psum x32, waiting for transfers between devices, panel_step(): diag_fac = lax.psum(jnp.where(is_owner, diag_own, 0.0), 'row')  1090 us
    another operation x192, other arithmetic, panel_step(): jnp.linalg.cholesky(jnp.where(is_owner, diag_blk, eye_blk))  1090 us
    psum x32, waiting for transfers between devices, transposed_panel(): return lax.psum(spread, 'row')  1070 us
    psum x32, waiting for transfers between devices, panel_step(): lax.psum(jnp.where(below_mask & own_col, solved_blocks, 0.0).astype(jnp.b...  930 us
    another operation x124, other arithmetic, panel_step(): lax.linalg.triangular_solve(diag_fac, col_blk, left_side=False, lower=Tru...  653 us
    while x176, local copies, waits for them, and re-layouts  476 us
    dot_general x32, matrix products, panel_step(): lax.dot_general(row_panel.reshape(win_rows, blk_size), col_panel.reshape(...  211 us
    another operation x320, local copies, waits for them, and re-layouts  135 us
  transfers between devices with their start and end apart: 96, of which 96 were waited for; matrix products, arithmetic and copies ran while one was open for 7% of the time, Pallas kernels for 0%

commit v1 on v0

v1 whole, which is shorter than its diff:
```python
import functools

import jax
import jax.numpy as jnp
from jax import lax
from jax.experimental import pallas as pl
from jax.experimental.pallas import tpu as pltpu
from jax.sharding import PartitionSpec as P

MESH = pl.DeviceIdType.MESH
HIGH = lax.Precision.HIGHEST
GRID = 4
BLK = 256
HALF = 128
PAN = 16
SLOTS = 4
F32, B16 = jnp.float32, jnp.bfloat16
NT = (((1,), (1,)), ((), ()))
TN = (((0,), (0,)), ((), ()))


def split3(x):
    hi = x.astype(B16)
    rest = x - hi.astype(F32)
    mid = rest.astype(B16)
    return hi, mid, (rest - mid.astype(F32)).astype(B16)


def gram(left, right):
    a1, a2, a3 = split3(left)
    b1, b2, b3 = split3(right)
    lhs = jnp.concatenate([a1, a1, a2, a2, a1, a3], axis=0)
    rhs = jnp.concatenate([b1, b2, b1, b2, b3, b1], axis=0)
    return lax.dot_general(lhs, rhs, TN, preferred_element_type=F32)


def eliminate(rows, base):
    groups = rows.shape[0]
    cols = [jnp.broadcast_to(rows[0][:, base + t : base + t + 1], (PAN, HALF))[None] for t in range(PAN)]
    work = jnp.concatenate(cols + [rows], axis=0)
    sub = lax.broadcasted_iota(jnp.int32, (PAN, HALF), 0)
    scale = jnp.zeros((PAN, HALF), F32)
    for t in range(PAN):
        root = jnp.broadcast_to(lax.rsqrt(work[0, t : t + 1, :]), (PAN, HALF))
        scale = jnp.where(sub == t, root, scale)
        mult = jnp.where(sub > t, work[0] * (root * root), 0.0)
        work = work[1:]
        work = work - mult[None] * work[:, t : t + 1, :]
    return work[-groups:] * scale[None]


def factor_half(tab):
    count = HALF // PAN
    groups = tab.shape[1] // HALF
    done = []
    for p in range(count):
        own = tab[:PAN]
        rows = jnp.concatenate([own[None, :, g * HALF : (g + 1) * HALF] for g in range(groups)], axis=0)
        out = eliminate(rows, p * PAN)
        flat = jnp.concatenate([out[g] for g in range(groups)], axis=1)
        done.append(flat)
        if p + 1 < count:
            tab = tab[PAN:] - gram(flat[:, :HALF], flat)[(p + 1) * PAN :]
    return jnp.concatenate(done, axis=0)


def kernel(nb, a_ref, o_ref, mat, row_pan, col_pan, inv_a, inv_b, load_sem, br_recv, bc_recv, row_send, chain_send,
           inv_recv, inv_send, row_free, inv_free, chain_free):
    r = lax.axis_index("row")
    c = lax.axis_index("col")
    steps = nb * GRID
    last = GRID * (nb - 1)

    def first_block(k, pos):
        return lax.div(k + GRID - pos, GRID)

    def rows_of(t):
        return pl.ds(pl.multiple_of(t * BLK, BLK), BLK)

    def load(t, s):
        return pltpu.make_async_copy(a_ref.at[t, :, pl.ds(s * BLK, BLK)], mat.at[s, pl.ds(t * BLK, BLK), :], load_sem.at[t, s])

    def store(t, s):
        return pltpu.make_async_copy(mat.at[s, pl.ds(t * BLK, BLK), :], o_ref.at[t, :, pl.ds(s * BLK, BLK)], load_sem.at[t, s])

    for s in range(nb):
        for t in range(nb):
            load(t, s).start()

    barrier = pltpu.get_barrier_semaphore()
    for off in range(1, GRID):
        pl.semaphore_signal(barrier, inc=1, device_id={"row": lax.rem(r + off, GRID)}, device_id_type=MESH)
        pl.semaphore_signal(barrier, inc=1, device_id={"col": lax.rem(c + off, GRID)}, device_id_type=MESH)
    pl.semaphore_wait(barrier, 2 * (GRID - 1))

    for s in range(nb):
        for t in range(nb):
            load(t, s).wait()

    def row_copy(slot, t, off):
        return pltpu.make_async_remote_copy(
            src_ref=row_pan.at[slot, rows_of(t), :], dst_ref=row_pan.at[slot, rows_of(t), :],
            send_sem=row_send.at[off - 1, t], recv_sem=br_recv.at[slot, t],
            device_id={"col": lax.rem(c + off, GRID)}, device_id_type=MESH)

    def chain_copy(src, slot, s, way):
        return pltpu.make_async_remote_copy(
            src_ref=src.at[slot, rows_of(s), :], dst_ref=col_pan.at[slot, rows_of(s), :],
            send_sem=chain_send.at[slot, way, s], recv_sem=bc_recv.at[slot, s],
            device_id={"row": r + 1 - 2 * way}, device_id_type=MESH)

    def inv_copy(off, part):
        ref = (inv_a, inv_b)[part]
        return pltpu.make_async_remote_copy(
            src_ref=ref, dst_ref=ref, send_sem=inv_send.at[off - 1, part], recv_sem=inv_recv.at[part],
            device_id={"row": lax.rem(r + off, GRID)}, device_id_type=MESH)

    def sends(way):
        return ((r >= c) & (r < GRID - 1)) if way == 0 else ((r <= c) & (r > 0))

    def pass_on(src, k, s):
        slot = lax.rem(k, SLOTS)
        for way in range(2):
            @pl.when(sends(way))
            def _():
                @pl.when((s == first_block(k, c)) & (k >= SLOTS))
                def _():
                    pl.semaphore_wait(chain_free.at[way], 1)
                chain_copy(src, slot, s, way).start()

    def own_col_block(k, s):
        slot = lax.rem(k, SLOTS)
        col_pan[slot, rows_of(s), :] = row_pan[slot, rows_of(s), :]
        pass_on(row_pan, k, s)

    def take_row(k, t):
        row_copy(lax.rem(k, SLOTS), t, 1).wait_recv()

        @pl.when(r == c)
        def _():
            own_col_block(k, t)

    def take_col(k, s):
        chain_copy(col_pan, lax.rem(k, SLOTS), s, 0).wait_recv()
        pass_on(col_pan, k, s)

    def update(k, t, s, count):
        slot = lax.rem(k, SLOTS)
        span = pl.ds(pl.multiple_of(t * BLK, BLK), count * BLK)
        prod = lax.dot_general(row_pan[slot, span, :], col_pan[slot, rows_of(s), :], NT, preferred_element_type=F32)
        mat[s, span, :] = mat[s, span, :] - prod

    def loop(lo, hi, body):
        def run(i, carry):
            body(i)
            return carry
        lax.fori_loop(lo, hi, run, 0)

    def factor_diag(k):
        t0 = lax.div(k, GRID)
        blk = mat[t0, rows_of(t0), :]
        eye = (lax.broadcasted_iota(jnp.int32, (HALF, HALF), 0) == lax.broadcasted_iota(jnp.int32, (HALF, HALF), 1)).astype(F32)

        def for_peers(act):
            for off in range(1, GRID):
                @pl.when(k < last + lax.rem(r + off, GRID))
                def _():
                    act(off)

        @pl.when(k >= GRID)
        def _():
            for_peers(lambda off: pl.semaphore_wait(inv_free.at[off - 1], 1))

        top = factor_half(jnp.concatenate([blk[:HALF], eye], axis=1))
        inv_a[...] = top[:, 2 * HALF :]
        for_peers(lambda off: inv_copy(off, 0).start())
        mid = lax.dot_general(top[:, HALF : 2 * HALF], top[:, HALF:], TN, precision=HIGH, preferred_element_type=F32)
        low = factor_half(jnp.concatenate([blk[HALF:, HALF:] - mid[:, :HALF], -mid[:, HALF:], eye], axis=1))
        inv_b[...] = low[:, HALF:]
        for_peers(lambda off: inv_copy(off, 1).start())
        zero = jnp.zeros((HALF, HALF), F32)
        up = lax.broadcasted_iota(jnp.int32, (HALF, HALF), 0) <= lax.broadcasted_iota(jnp.int32, (HALF, HALF), 1)
        left = jnp.concatenate([jnp.where(up, top[:, :HALF], 0.0).T, top[:, HALF : 2 * HALF].T], axis=0)
        right = jnp.concatenate([zero, jnp.where(up, low[:, :HALF], 0.0).T], axis=0)
        mat[t0, rows_of(t0), :] = jnp.concatenate([left, right], axis=1)

    def solve_col(k):
        t0 = lax.div(k, GRID)
        slot = lax.rem(k, SLOTS)

        @pl.when(k < last + r)
        def _():
            @pl.when(r != c)
            def _():
                inv_copy(1, 0).wait_recv()
                inv_copy(1, 1).wait_recv()

            @pl.when(k >= SLOTS)
            def _():
                pl.semaphore_wait(row_free, GRID - 1)

        def one(t):
            inv = jnp.concatenate(
                [jnp.concatenate([inv_a[...], jnp.zeros((HALF, HALF), F32)], axis=1), inv_b[...]], axis=0)
            sol = lax.dot_general(mat[t0, rows_of(t), :], inv, NT, precision=HIGH, preferred_element_type=F32)
            mat[t0, rows_of(t), :] = sol
            row_pan[slot, rows_of(t), :] = sol.astype(B16)
            for off in range(1, GRID):
                row_copy(slot, t, off).start()

            @pl.when(r == c)
            def _():
                own_col_block(k, t)

        loop(first_block(k, r), nb, one)

        @pl.when(r == c)
        def _():
            for off in range(1, GRID):
                @pl.when(k < last + lax.rem(r + off, GRID))
                def _():
                    inv_copy(off, 0).wait_send()
                    inv_copy(off, 1).wait_send()

        @pl.when((r != c) & (k + GRID < last + r))
        def _():
            pl.semaphore_signal(inv_free.at[lax.rem(r - c + GRID, GRID) - 1], inc=1, device_id={"row": lax.rem(k, GRID)}, device_id_type=MESH)

    def trail(k):
        d = lax.rem(k, GRID)
        nxt = lax.rem(k + 1, GRID)
        t_lo = first_block(k, r)
        s_lo = first_block(k, c) + jnp.where(c == nxt, 1, 0)

        @pl.when((c != d) & (c != nxt))
        def _():
            loop(t_lo, nb, lambda t: take_row(k, t))

        @pl.when(r != c)
        def _():
            loop(s_lo, nb, lambda s: take_col(k, s))

        def column(s):
            lo = jnp.maximum(t_lo, s)
            pairs = lax.div(nb - lo, 2)
            loop(0, pairs, lambda q: update(k, lo + 2 * q, s, 2))

            @pl.when(lax.rem(nb - lo, 2) == 1)
            def _():
                update(k, nb - 1, s, 1)

        loop(s_lo, nb, column)

    def finish(k):
        d = lax.rem(k, GRID)

        @pl.when(c == d)
        def _():
            def one(t):
                for off in range(1, GRID):
                    row_copy(lax.rem(k, SLOTS), t, off).wait_send()
            loop(first_block(k, r), nb, one)

        for way in range(2):
            @pl.when(sends(way))
            def _():
                loop(first_block(k, c), nb, lambda s: chain_copy(col_pan, lax.rem(k, SLOTS), s, way).wait_send())

        @pl.when((c != d) & (k + SLOTS < last + r))
        def _():
            pl.semaphore_signal(row_free, inc=1, device_id={"col": d}, device_id_type=MESH)

        for way in range(2):
            @pl.when((k + SLOTS < last + c) & ((r > c) if way == 0 else (r < c)))
            def _():
                pl.semaphore_signal(chain_free.at[way], inc=1, device_id={"row": r - 1 + 2 * way}, device_id_type=MESH)

    def ahead(k):
        s1 = lax.div(k + 1, GRID)

        @pl.when(r == c)
        def _():
            take_row(k, s1)
            update(k, s1, s1, 1)

        @pl.when(r != c)
        def _():
            take_col(k, s1)

            def one(t):
                take_row(k, t)
                update(k, t, s1, 1)
            loop(first_block(k, r), nb, one)

    def ahead_rest(k):
        s1 = lax.div(k + 1, GRID)

        def one(t):
            take_row(k, t)
            update(k, t, s1, 1)
        loop(s1 + 1, nb, one)

    def step(k):
        d = lax.rem(k, GRID)

        @pl.when(c == d)
        def _():
            @pl.when(r == d)
            def _():
                factor_diag(k)

                @pl.when(k > 0)
                def _():
                    ahead_rest(k - 1)
            solve_col(k)

        @pl.when(k > 0)
        def _():
            trail(k - 1)

        @pl.when(k > 1)
        def _():
            finish(k - 2)

        @pl.when((c == lax.rem(k + 1, GRID)) & (k + 1 < steps))
        def _():
            ahead(k)

    loop(0, steps, step)
    finish(steps - 2)

    for s in range(nb):
        for t in range(nb):
            store(t, s).start()
    for s in range(nb):
        for t in range(nb):
            store(t, s).wait()


def solution(mesh):
    def factor_local(a_loc):
        nb, blk, width = a_loc.shape
        dma = pltpu.SemaphoreType.DMA
        reg = pltpu.SemaphoreType.REGULAR
        work = pl.pallas_call(
            functools.partial(kernel, nb),
            out_shape=jax.ShapeDtypeStruct(a_loc.shape, F32),
            in_specs=[pl.BlockSpec(memory_space=pl.ANY)],
            out_specs=pl.BlockSpec(memory_space=pl.ANY),
            scratch_shapes=[
                pltpu.VMEM((nb, nb * blk, blk), F32),
                pltpu.VMEM((SLOTS, nb * blk, blk), B16),
                pltpu.VMEM((SLOTS, nb * blk, blk), B16),
                pltpu.VMEM((HALF, HALF), F32),
                pltpu.VMEM((HALF, BLK), F32),
                dma((nb, nb)),
                dma((SLOTS, nb)),
                dma((SLOTS, nb)),
                dma((GRID - 1, nb)),
                dma((SLOTS, 2, nb)),
                dma((2,)),
                dma((GRID - 1, 2)),
                reg,
                reg((GRID - 1,)),
                reg((2,)),
            ],
            compiler_params=pltpu.CompilerParams(collective_id=0, has_side_effects=True, vmem_limit_bytes=56 * 1024 * 1024),
        )(a_loc)
        row_id = lax.axis_index("row")
        col_id = lax.axis_index("col")
        row_blk = jnp.arange(nb) * GRID + row_id
        col_blk = jnp.arange(width // blk) * GRID + col_id
        keep = row_blk[:, None, None, None] >= col_blk[None, None, :, None]
        return jnp.where(keep, work.reshape(nb, blk, width // blk, blk), 0.0).reshape(nb, blk, width)

    spec = P(("batch", "row"), None, "col")
    return jax.shard_map(factor_local, mesh=mesh, in_specs=(spec,), out_specs=spec, check_vma=False)
```

time: 6460 us -> 630 us (0.10)
  waiting for transfers between devices: 3100 us -> 0 us
  other arithmetic: 1980 us -> 12.3 us
  local copies, waits for them, and re-layouts: 867 us -> 0.08 us
  Pallas kernels: 0 us -> 614 us
  matrix products: 338 us -> 0 us
  loops' own time: 120 us -> 0 us
    psum x96 -> x0, waiting for transfers between devices: 3100 us -> none  [the longest x32 1090 us: panel_step(): diag_fac = lax.psum(jnp.where(is_owner, diag_own, 0.0), 'row')]
    another operation x316 -> x0, other arithmetic: 1740 us -> none  [the longest x192 1090 us: panel_step(): jnp.linalg.cholesky(jnp.where(is_owner, diag_blk, eye_blk))]
    pallas_call x0 -> x1, Pallas kernels: none -> 614 us  [factor_local(): pl.pallas_call(functools.partial(kernel, nb), out_shape=jax.ShapeDtypeStr...]
    while x176 -> x0, local copies, waits for them, and re-layouts: 476 us -> none
    dot_general x32 -> x0, matrix products: 211 us -> none  [panel_step(): lax.dot_general(row_panel.reshape(win_rows, blk_size), col_panel.reshape(...]
    another operation x592 -> x0, local copies, waits for them, and re-layouts: 160 us -> none
    another operation x160 -> x0, matrix products: 126 us -> none  [the longest x96 111 us: panel_step(): lax.linalg.triangular_solve(diag_fac, col_blk, left_side=False, lower=Tru...]
    another operation x40 -> x0, loops' own time: 120 us -> none  [the longest x8 118 us: factor_local(): lax.fori_loop(bounds[phase_idx], bounds[phase_idx + 1], panel_step, work_...]
  transfers between devices with their start and end apart: 96 -> 0, of which waited for: 96 -> 0; matrix products, arithmetic and copies ran while one was open for 7% -> 0% of each run, Pallas kernels for 0% -> 0%
where the time goes in v1:
time: 630 us; the launch traced here: 626 us
  Pallas kernels  614 us (97%)
  other arithmetic  12.3 us (2%)
    pallas_call x1, Pallas kernels, factor_local(): pl.pallas_call(functools.partial(kernel, nb), out_shape=jax.ShapeDtypeStr...  614 us

profile of v1, /device:TPU:31, one launch (start us, length us, event | category | flops | bytes accessed | tf_op | source)
XLA Modules:
  0.0 626.2 jit_solution(17855557052297512430)
XLA Ops:
  0.0 0.1 broadcast_compare_fusion
  0.1 0.1 broadcast_in_dim.18
  0.2 613.8 %shard_map.17 = f32[8,256,2048]{2,1,0:T(8,128)} custom-call(f32[8,256,2048]{2,1,0:T(8,128)} %a_ref.1), custom_call_target="tpu_custom_call" | custom-call | tf_op jit(solution)/shard_map/pallas_call | solution.py:345
  614.0 12.3 %broadcast_select_fusion = f32[8,256,2048]{2,1,0:T(8,128)} fusion(f32[8,256,2048]{2,1,0:T(8,128)} %shard_map.17, pred[8,2048]{1,0:T(8,128)(4,1)S(1)} %bitcast.1), kind=kLoop, calls=%fused_computation | loop fusion | flops 4194304 | bytes 33570816 | tf_op jit(solution)/shard_map/jit(_where)/select_n | solution.py:374
  (1 shorter events, 0.0 us)

commit v2 on v1

--- a/solution.py
+++ b/solution.py
@@ -49,7 +49,7 @@
     return work[-groups:] * scale[None]
 
 
-def factor_half(tab):
+def factor_half(tab, emit):
     count = HALF // PAN
     groups = tab.shape[1] // HALF
     done = []
@@ -59,13 +59,14 @@
         out = eliminate(rows, p * PAN)
         flat = jnp.concatenate([out[g] for g in range(groups)], axis=1)
         done.append(flat)
+        emit(p, flat)
         if p + 1 < count:
             tab = tab[PAN:] - gram(flat[:, :HALF], flat)[(p + 1) * PAN :]
     return jnp.concatenate(done, axis=0)
 
 
-def kernel(nb, a_ref, o_ref, mat, row_pan, col_pan, inv_a, inv_b, load_sem, br_recv, bc_recv, row_send, chain_send,
-           inv_recv, inv_send, row_free, inv_free, chain_free):
+def kernel(nb, a_ref, o_ref, mat, row_pan, col_pan, inv_a, inv_b, nxt_a, nxt_b, nxt_x, load_sem, br_recv, bc_recv,
+           row_send, chain_send, inv_recv, inv_send, nxt_recv, x_recv, x_send, row_free, inv_free, chain_free, nxt_free, x_free):
     r = lax.axis_index("row")
     c = lax.axis_index("col")
     steps = nb * GRID
@@ -81,7 +82,7 @@
         return pltpu.make_async_copy(a_ref.at[t, :, pl.ds(s * BLK, BLK)], mat.at[s, pl.ds(t * BLK, BLK), :], load_sem.at[t, s])
 
     def store(t, s):
-        return pltpu.make_async_copy(mat.at[s, pl.ds(t * BLK, BLK), :], o_ref.at[t, :, pl.ds(s * BLK, BLK)], load_sem.at[t, s])
+        return pltpu.make_async_copy(mat.at[s, pl.ds(t * BLK, BLK), :], o_ref.at[t, :, pl.ds(pl.multiple_of(s * BLK, BLK), BLK)], load_sem.at[t, s])
 
     for s in range(nb):
         for t in range(nb):
@@ -91,11 +92,12 @@
     for off in range(1, GRID):
         pl.semaphore_signal(barrier, inc=1, device_id={"row": lax.rem(r + off, GRID)}, device_id_type=MESH)
         pl.semaphore_signal(barrier, inc=1, device_id={"col": lax.rem(c + off, GRID)}, device_id_type=MESH)
-    pl.semaphore_wait(barrier, 2 * (GRID - 1))
-
-    for s in range(nb):
-        for t in range(nb):
-            load(t, s).wait()
+    for off in (1, GRID - 1):
+        pl.semaphore_signal(barrier, inc=1, device_id={"row": lax.rem(r + off, GRID), "col": lax.rem(c + off, GRID)}, device_id_type=MESH)
+    pl.semaphore_wait(barrier, 2 * GRID)
+
+    for t in range(nb):
+        load(t, 0).wait()
 
     def row_copy(slot, t, off):
         return pltpu.make_async_remote_copy(
@@ -109,11 +111,29 @@
             send_sem=chain_send.at[slot, way, s], recv_sem=bc_recv.at[slot, s],
             device_id={"row": r + 1 - 2 * way}, device_id_type=MESH)
 
+    def inv_part(a, b, part):
+        return a if part == 0 else b.at[pl.ds((part - 1) * (HALF // 2), HALF // 2), :]
+
     def inv_copy(off, part):
-        ref = (inv_a, inv_b)[part]
+        ref = inv_part(inv_a, inv_b, part)
         return pltpu.make_async_remote_copy(
-            src_ref=ref, dst_ref=ref, send_sem=inv_send.at[off - 1, part], recv_sem=inv_recv.at[part],
+            src_ref=ref, dst_ref=ref, send_sem=inv_send.at[off, part], recv_sem=inv_recv.at[part],
             device_id={"row": lax.rem(r + off, GRID)}, device_id_type=MESH)
+
+    def nxt_copy(part):
+        return pltpu.make_async_remote_copy(
+            src_ref=inv_part(inv_a, inv_b, part), dst_ref=inv_part(nxt_a, nxt_b, part),
+            send_sem=inv_send.at[0, part], recv_sem=nxt_recv.at[part],
+            device_id={"row": lax.rem(r + 1, GRID), "col": lax.rem(c + 1, GRID)}, device_id_type=MESH)
+
+    def x_copy(k):
+        return pltpu.make_async_remote_copy(
+            src_ref=mat.at[lax.div(k, GRID), rows_of(lax.div(k + 1, GRID)), :], dst_ref=nxt_x,
+            send_sem=x_send, recv_sem=x_recv,
+            device_id={"col": lax.rem(c + 1, GRID)}, device_id_type=MESH)
+
+    def gather_inv(a, b):
+        return jnp.concatenate([jnp.concatenate([a[...], jnp.zeros((HALF, HALF), F32)], axis=1), b[...]], axis=0)
 
     def sends(way):
         return ((r >= c) & (r < GRID - 1)) if way == 0 else ((r <= c) & (r > 0))
@@ -171,19 +191,42 @@
         def _():
             for_peers(lambda off: pl.semaphore_wait(inv_free.at[off - 1], 1))
 
-        top = factor_half(jnp.concatenate([blk[:HALF], eye], axis=1))
-        inv_a[...] = top[:, 2 * HALF :]
-        for_peers(lambda off: inv_copy(off, 0).start())
+            @pl.when(k + 1 < steps)
+            def _():
+                pl.semaphore_wait(nxt_free, 1)
+
+        def send(part):
+            @pl.when(k + 1 < steps)
+            def _():
+                nxt_copy(part).start()
+            for_peers(lambda off: inv_copy(off, part).start())
+
+        def emit_top(p, flat):
+            inv_a[p * PAN : (p + 1) * PAN, :] = flat[:, 2 * HALF :]
+            if p == HALF // PAN - 1:
+                send(0)
+
+        def emit_low(p, flat):
+            inv_b[p * PAN : (p + 1) * PAN, :] = flat[:, HALF:]
+            if (p + 1) % (HALF // PAN // 2) == 0:
+                send(2 * (p + 1) // (HALF // PAN))
+
+        top = factor_half(jnp.concatenate([blk[:HALF], eye], axis=1), emit_top)
         mid = lax.dot_general(top[:, HALF : 2 * HALF], top[:, HALF:], TN, precision=HIGH, preferred_element_type=F32)
-        low = factor_half(jnp.concatenate([blk[HALF:, HALF:] - mid[:, :HALF], -mid[:, HALF:], eye], axis=1))
-        inv_b[...] = low[:, HALF:]
-        for_peers(lambda off: inv_copy(off, 1).start())
+        low = factor_half(jnp.concatenate([blk[HALF:, HALF:] - mid[:, :HALF], -mid[:, HALF:], eye], axis=1), emit_low)
         zero = jnp.zeros((HALF, HALF), F32)
         up = lax.broadcasted_iota(jnp.int32, (HALF, HALF), 0) <= lax.broadcasted_iota(jnp.int32, (HALF, HALF), 1)
         left = jnp.concatenate([jnp.where(up, top[:, :HALF], 0.0).T, top[:, HALF : 2 * HALF].T], axis=0)
         right = jnp.concatenate([zero, jnp.where(up, low[:, :HALF], 0.0).T], axis=0)
         mat[t0, rows_of(t0), :] = jnp.concatenate([left, right], axis=1)
 
+    def for_row(k, t, act):
+        @pl.when((r != lax.rem(k + 1, GRID)) | (t != lax.div(k + 1, GRID)))
+        def _():
+            act(1)
+        for off in range(2, GRID):
+            act(off)
+
     def solve_col(k):
         t0 = lax.div(k, GRID)
         slot = lax.rem(k, SLOTS)
@@ -192,21 +235,25 @@
         def _():
             @pl.when(r != c)
             def _():
-                inv_copy(1, 0).wait_recv()
-                inv_copy(1, 1).wait_recv()
+                for part in range(3):
+                    inv_copy(1, part).wait_recv()
 
             @pl.when(k >= SLOTS)
             def _():
                 pl.semaphore_wait(row_free, GRID - 1)
 
+        early = (r == lax.rem(k + 1, GRID)) & (k + 1 < steps)
+
+        @pl.when(early)
+        def _():
+            x_copy(k).wait_send()
+
         def one(t):
-            inv = jnp.concatenate(
-                [jnp.concatenate([inv_a[...], jnp.zeros((HALF, HALF), F32)], axis=1), inv_b[...]], axis=0)
+            inv = gather_inv(inv_a, inv_b)
             sol = lax.dot_general(mat[t0, rows_of(t), :], inv, NT, precision=HIGH, preferred_element_type=F32)
             mat[t0, rows_of(t), :] = sol
             row_pan[slot, rows_of(t), :] = sol.astype(B16)
-            for off in range(1, GRID):
-                row_copy(slot, t, off).start()
+            for_row(k, t, lambda off: row_copy(slot, t, off).start())
 
             @pl.when(r == c)
             def _():
@@ -219,46 +266,55 @@
             for off in range(1, GRID):
                 @pl.when(k < last + lax.rem(r + off, GRID))
                 def _():
-                    inv_copy(off, 0).wait_send()
-                    inv_copy(off, 1).wait_send()
+                    for part in range(3):
+                        inv_copy(off, part).wait_send()
+
+            @pl.when(k + 1 < steps)
+            def _():
+                for part in range(3):
+                    nxt_copy(part).wait_send()
 
         @pl.when((r != c) & (k + GRID < last + r))
         def _():
             pl.semaphore_signal(inv_free.at[lax.rem(r - c + GRID, GRID) - 1], inc=1, device_id={"row": lax.rem(k, GRID)}, device_id_type=MESH)
+
+    def columns(k, lo, hi):
+        def column(s):
+            first = jnp.maximum(first_block(k, r), s)
+            pairs = lax.div(nb - first, 2)
+            loop(0, pairs, lambda q: update(k, first + 2 * q, s, 2))
+
+            @pl.when(lax.rem(nb - first, 2) == 1)
+            def _():
+                update(k, nb - 1, s, 1)
+
+        @pl.when(r != c)
+        def _():
+            loop(lo, hi, lambda s: take_col(k, s))
+        loop(lo, hi, column)
 
     def trail(k):
         d = lax.rem(k, GRID)
         nxt = lax.rem(k + 1, GRID)
-        t_lo = first_block(k, r)
+        soon = (c == lax.rem(k + 2, GRID)) & (k + 2 < steps)
         s_lo = first_block(k, c) + jnp.where(c == nxt, 1, 0)
 
         @pl.when((c != d) & (c != nxt))
         def _():
-            loop(t_lo, nb, lambda t: take_row(k, t))
-
-        @pl.when(r != c)
-        def _():
-            loop(s_lo, nb, lambda s: take_col(k, s))
-
-        def column(s):
-            lo = jnp.maximum(t_lo, s)
-            pairs = lax.div(nb - lo, 2)
-            loop(0, pairs, lambda q: update(k, lo + 2 * q, s, 2))
-
-            @pl.when(lax.rem(nb - lo, 2) == 1)
-            def _():
-                update(k, nb - 1, s, 1)
-
-        loop(s_lo, nb, column)
+            loop(first_block(k, r), nb, lambda t: take_row(k, t))
+
+        columns(k, s_lo, jnp.where(soon, s_lo + 1, nb))
 
     def finish(k):
         d = lax.rem(k, GRID)
 
         @pl.when(c == d)
         def _():
+            for t in range(nb):
+                store(t, lax.div(k, GRID)).start()
+
             def one(t):
-                for off in range(1, GRID):
-                    row_copy(lax.rem(k, SLOTS), t, off).wait_send()
+                for_row(k, t, lambda off: row_copy(lax.rem(k, SLOTS), t, off).wait_send())
             loop(first_block(k, r), nb, one)
 
         for way in range(2):
@@ -280,8 +336,20 @@
 
         @pl.when(r == c)
         def _():
-            take_row(k, s1)
-            update(k, s1, s1, 1)
+            slot = lax.rem(k, SLOTS)
+            x_copy(k).wait_recv()
+            for part in range(3):
+                nxt_copy(part).wait_recv()
+            sol = lax.dot_general(nxt_x[...], gather_inv(nxt_a, nxt_b), NT, precision=HIGH, preferred_element_type=F32).astype(B16)
+            row_pan[slot, rows_of(s1), :] = sol
+            col_pan[slot, rows_of(s1), :] = sol
+            mat[s1, rows_of(s1), :] = mat[s1, rows_of(s1), :] - lax.dot_general(sol, sol, NT, preferred_element_type=F32)
+            pass_on(row_pan, k, s1)
+
+            @pl.when(k + GRID + 1 < steps)
+            def _():
+                pl.semaphore_signal(x_free, inc=1, device_id={"col": lax.rem(k, GRID)}, device_id_type=MESH)
+                pl.semaphore_signal(nxt_free, inc=1, device_id={"row": lax.rem(k, GRID), "col": lax.rem(k, GRID)}, device_id_type=MESH)
 
         @pl.when(r != c)
         def _():
@@ -290,6 +358,13 @@
             def one(t):
                 take_row(k, t)
                 update(k, t, s1, 1)
+
+                @pl.when((r == lax.rem(k + 2, GRID)) & (t == lax.div(k + 2, GRID)) & (k + 2 < steps))
+                def _():
+                    @pl.when(k + 1 >= GRID)
+                    def _():
+                        pl.semaphore_wait(x_free, 1)
+                    x_copy(k + 1).start()
             loop(first_block(k, r), nb, one)
 
     def ahead_rest(k):
@@ -314,6 +389,16 @@
                     ahead_rest(k - 1)
             solve_col(k)
 
+            @pl.when(k > 1)
+            def _():
+                columns(k - 2, lax.div(k, GRID) + 1, nb)
+
+        @pl.when(k == 1)
+        def _():
+            for s in range(1, nb):
+                for t in range(nb):
+                    load(t, s).wait()
+
         @pl.when(k > 0)
         def _():
             trail(k - 1)
@@ -325,13 +410,15 @@
         @pl.when((c == lax.rem(k + 1, GRID)) & (k + 1 < steps))
         def _():
             ahead(k)
+
+    @pl.when((r == 1) & (c == 0))
+    def _():
+        x_copy(0).start()
 
     loop(0, steps, step)
     finish(steps - 2)
-
-    for s in range(nb):
-        for t in range(nb):
-            store(t, s).start()
+    finish(steps - 1)
+
     for s in range(nb):
         for t in range(nb):
             store(t, s).wait()
@@ -353,16 +440,24 @@
                 pltpu.VMEM((SLOTS, nb * blk, blk), B16),
                 pltpu.VMEM((HALF, HALF), F32),
                 pltpu.VMEM((HALF, BLK), F32),
+                pltpu.VMEM((HALF, HALF), F32),
+                pltpu.VMEM((HALF, BLK), F32),
+                pltpu.VMEM((BLK, BLK), F32),
                 dma((nb, nb)),
                 dma((SLOTS, nb)),
                 dma((SLOTS, nb)),
                 dma((GRID - 1, nb)),
                 dma((SLOTS, 2, nb)),
-                dma((2,)),
-                dma((GRID - 1, 2)),
+                dma((3,)),
+                dma((GRID, 3)),
+                dma((3,)),
+                dma,
+                dma,
                 reg,
                 reg((GRID - 1,)),
                 reg((2,)),
+                reg,
+                reg,
             ],
             compiler_params=pltpu.CompilerParams(collective_id=0, has_side_effects=True, vmem_limit_bytes=56 * 1024 * 1024),
         )(a_loc)

time: 630 us -> 628 us (level)
  no operation moved by 1% of the time
where the time goes in v2:
time: 628 us; the launch traced here: 625 us
  Pallas kernels  612 us (97%)
  other arithmetic  12.4 us (2%)
    pallas_call x1, Pallas kernels, factor_local(): pl.pallas_call(functools.partial(kernel, nb), out_shape=jax.ShapeDtypeStr...  612 us

profile of v2, /device:TPU:31, one launch (start us, length us, event | category | flops | bytes accessed | tf_op | source)
XLA Modules:
  0.0 624.6 jit_solution(11843306391985052953)
XLA Ops:
  0.0 0.1 broadcast_compare_fusion
  0.1 0.1 broadcast_in_dim.18
  0.2 612.2 %shard_map.17 = f32[8,256,2048]{2,1,0:T(8,128)} custom-call(f32[8,256,2048]{2,1,0:T(8,128)} %a_ref.1), custom_call_target="tpu_custom_call" | custom-call | tf_op jit(solution)/shard_map/pallas_call | solution.py:432
  612.4 12.3 %broadcast_select_fusion = f32[8,256,2048]{2,1,0:T(8,128)} fusion(f32[8,256,2048]{2,1,0:T(8,128)} %shard_map.17, pred[8,2048]{1,0:T(8,128)(4,1)S(1)} %bitcast.1), kind=kLoop, calls=%fused_computation | loop fusion | flops 4194304 | bytes 33570816 | tf_op jit(solution)/shard_map/jit(_where)/select_n | solution.py:469
  (1 shorter events, 0.0 us)

commit v3 on v2

--- a/solution.py
+++ b/solution.py
@@ -66,7 +66,7 @@
 
 
 def kernel(nb, a_ref, o_ref, mat, row_pan, col_pan, inv_a, inv_b, nxt_a, nxt_b, nxt_x, load_sem, br_recv, bc_recv,
-           row_send, chain_send, inv_recv, inv_send, nxt_recv, x_recv, x_send, row_free, inv_free, chain_free, nxt_free, x_free):
+           row_send, relay_send, chain_send, inv_recv, inv_send, nxt_recv, x_recv, x_send, row_free, inv_free, chain_free, nxt_free, x_free):
     r = lax.axis_index("row")
     c = lax.axis_index("col")
     steps = nb * GRID
@@ -105,6 +105,15 @@
             send_sem=row_send.at[off - 1, t], recv_sem=br_recv.at[slot, t],
             device_id={"col": lax.rem(c + off, GRID)}, device_id_type=MESH)
 
+    def relay_copy(slot, t):
+        return pltpu.make_async_remote_copy(
+            src_ref=row_pan.at[slot, rows_of(t), :], dst_ref=row_pan.at[slot, rows_of(t), :],
+            send_sem=relay_send.at[slot, t], recv_sem=br_recv.at[slot, t],
+            device_id={"col": lax.rem(c + 1, GRID)}, device_id_type=MESH)
+
+    def relays(k):
+        return (lax.rem(c, 2) == 0) & (lax.div(c, 2) != lax.div(lax.rem(k, GRID), 2))
+
     def chain_copy(src, slot, s, way):
         return pltpu.make_async_remote_copy(
             src_ref=src.at[slot, rows_of(s), :], dst_ref=col_pan.at[slot, rows_of(s), :],
@@ -114,11 +123,17 @@
     def inv_part(a, b, part):
         return a if part == 0 else b.at[pl.ds((part - 1) * (HALF // 2), HALF // 2), :]
 
-    def inv_copy(off, part):
+    def inv_copy(way, part):
         ref = inv_part(inv_a, inv_b, part)
         return pltpu.make_async_remote_copy(
-            src_ref=ref, dst_ref=ref, send_sem=inv_send.at[off, part], recv_sem=inv_recv.at[part],
-            device_id={"row": lax.rem(r + off, GRID)}, device_id_type=MESH)
+            src_ref=ref, dst_ref=ref, send_sem=inv_send.at[1 + way, part], recv_sem=inv_recv.at[part],
+            device_id={"row": r + 1 - 2 * way}, device_id_type=MESH)
+
+    def inv_ways(k, act):
+        for way in range(2):
+            @pl.when(sends(way) & (k < last + r + 1 - 2 * way))
+            def _():
+                act(way)
 
     def nxt_copy(part):
         return pltpu.make_async_remote_copy(
@@ -155,6 +170,10 @@
 
     def take_row(k, t):
         row_copy(lax.rem(k, SLOTS), t, 1).wait_recv()
+
+        @pl.when(relays(k))
+        def _():
+            relay_copy(lax.rem(k, SLOTS), t).start()
 
         @pl.when(r == c)
         def _():
@@ -199,7 +218,7 @@
             @pl.when(k + 1 < steps)
             def _():
                 nxt_copy(part).start()
-            for_peers(lambda off: inv_copy(off, part).start())
+            inv_ways(k, lambda way: inv_copy(way, part).start())
 
         def emit_top(p, flat):
             inv_a[p * PAN : (p + 1) * PAN, :] = flat[:, 2 * HALF :]
@@ -221,11 +240,20 @@
         mat[t0, rows_of(t0), :] = jnp.concatenate([left, right], axis=1)
 
     def for_row(k, t, act):
-        @pl.when((r != lax.rem(k + 1, GRID)) | (t != lax.div(k + 1, GRID)))
+        own = (r == lax.rem(k + 1, GRID)) & (t == lax.div(k + 1, GRID))
+        odd = lax.rem(c, 2)
+
+        @pl.when(jnp.logical_not(own))
         def _():
             act(1)
-        for off in range(2, GRID):
-            act(off)
+
+        @pl.when(odd == 1)
+        def _():
+            act(3)
+
+        @pl.when((odd == 0) | own)
+        def _():
+            act(2)
 
     def solve_col(k):
         t0 = lax.div(k, GRID)
@@ -236,7 +264,8 @@
             @pl.when(r != c)
             def _():
                 for part in range(3):
-                    inv_copy(1, part).wait_recv()
+                    inv_copy(0, part).wait_recv()
+                    inv_ways(k, lambda way: inv_copy(way, part).start())
 
             @pl.when(k >= SLOTS)
             def _():
@@ -249,6 +278,10 @@
             x_copy(k).wait_send()
 
         def one(t):
+            @pl.when((k > 0) & ((t > first_block(k, r)) | (r == c)))
+            def _():
+                take_row(k - 1, t)
+                update(k - 1, t, t0, 1)
             inv = gather_inv(inv_a, inv_b)
             sol = lax.dot_general(mat[t0, rows_of(t), :], inv, NT, precision=HIGH, preferred_element_type=F32)
             mat[t0, rows_of(t), :] = sol
@@ -261,18 +294,15 @@
 
         loop(first_block(k, r), nb, one)
 
-        @pl.when(r == c)
-        def _():
-            for off in range(1, GRID):
-                @pl.when(k < last + lax.rem(r + off, GRID))
-                def _():
-                    for part in range(3):
-                        inv_copy(off, part).wait_send()
-
-            @pl.when(k + 1 < steps)
-            def _():
-                for part in range(3):
-                    nxt_copy(part).wait_send()
+        @pl.when((k < last + r) | (r == c))
+        def _():
+            for part in range(3):
+                inv_ways(k, lambda way: inv_copy(way, part).wait_send())
+
+        @pl.when((r == c) & (k + 1 < steps))
+        def _():
+            for part in range(3):
+                nxt_copy(part).wait_send()
 
         @pl.when((r != c) & (k + GRID < last + r))
         def _():
@@ -316,6 +346,11 @@
             def one(t):
                 for_row(k, t, lambda off: row_copy(lax.rem(k, SLOTS), t, off).wait_send())
             loop(first_block(k, r), nb, one)
+
+        @pl.when(relays(k))
+        def _():
+            made = (r == c) & (c == lax.rem(k + 1, GRID)) & (k + 1 < steps)
+            loop(first_block(k, r) + jnp.where(made, 1, 0), nb, lambda t: relay_copy(lax.rem(k, SLOTS), t).wait_send())
 
         for way in range(2):
             @pl.when(sends(way))
@@ -355,25 +390,19 @@
         def _():
             take_col(k, s1)
 
-            def one(t):
+            t = first_block(k, r)
+
+            @pl.when(t < nb)
+            def _():
                 take_row(k, t)
                 update(k, t, s1, 1)
 
-                @pl.when((r == lax.rem(k + 2, GRID)) & (t == lax.div(k + 2, GRID)) & (k + 2 < steps))
+                @pl.when((r == lax.rem(k + 2, GRID)) & (k + 2 < steps))
                 def _():
                     @pl.when(k + 1 >= GRID)
                     def _():
                         pl.semaphore_wait(x_free, 1)
                     x_copy(k + 1).start()
-            loop(first_block(k, r), nb, one)
-
-    def ahead_rest(k):
-        s1 = lax.div(k + 1, GRID)
-
-        def one(t):
-            take_row(k, t)
-            update(k, t, s1, 1)
-        loop(s1 + 1, nb, one)
 
     def step(k):
         d = lax.rem(k, GRID)
@@ -383,10 +412,6 @@
             @pl.when(r == d)
             def _():
                 factor_diag(k)
-
-                @pl.when(k > 0)
-                def _():
-                    ahead_rest(k - 1)
             solve_col(k)
 
             @pl.when(k > 1)
@@ -447,9 +472,10 @@
                 dma((SLOTS, nb)),
                 dma((SLOTS, nb)),
                 dma((GRID - 1, nb)),
+                dma((SLOTS, nb)),
                 dma((SLOTS, 2, nb)),
                 dma((3,)),
-                dma((GRID, 3)),
+                dma((3, 3)),
                 dma((3,)),
                 dma,
                 dma,

time: 628 us -> 583 us (0.928)
  Pallas kernels: 612 us -> 567 us
    pallas_call x1, Pallas kernels: 612 us -> 567 us  [factor_local(): pl.pallas_call(functools.partial(kernel, nb), out_shape=jax.ShapeDtypeStr...]
where the time goes in v3:
time: 583 us; the launch traced here: 579 us
  Pallas kernels  567 us (97%)
  other arithmetic  12.3 us (2%)
    pallas_call x1, Pallas kernels, factor_local(): pl.pallas_call(functools.partial(kernel, nb), out_shape=jax.ShapeDtypeStr...  567 us
    select_n x1, other arithmetic, factor_local(): jnp.where(keep, work.reshape(nb, blk, width // blk, blk), 0.0)  12.3 us

profile of v3, /device:TPU:31, one launch (start us, length us, event | category | flops | bytes accessed | tf_op | source)
XLA Modules:
  0.0 579.1 jit_solution(6249605743196433174)
XLA Ops:
  0.0 0.1 broadcast_compare_fusion
  0.1 0.1 broadcast_in_dim.18
  0.2 566.7 %shard_map.17 = f32[8,256,2048]{2,1,0:T(8,128)} custom-call(f32[8,256,2048]{2,1,0:T(8,128)} %a_ref.1), custom_call_target="tpu_custom_call" | custom-call | tf_op jit(solution)/shard_map/pallas_call | solution.py:457
  566.9 12.3 %broadcast_select_fusion = f32[8,256,2048]{2,1,0:T(8,128)} fusion(f32[8,256,2048]{2,1,0:T(8,128)} %shard_map.17, pred[8,2048]{1,0:T(8,128)(4,1)S(1)} %bitcast.1), kind=kLoop, calls=%fused_computation | loop fusion | flops 4194304 | bytes 33570816 | tf_op jit(solution)/shard_map/jit(_where)/select_n | solution.py:495
  (1 shorter events, 0.0 us)

commit v4 on v3

--- a/solution.py
+++ b/solution.py
@@ -13,7 +13,7 @@
 BLK = 256
 HALF = 128
 PAN = 16
-SLOTS = 4
+SLOTS = 8
 F32, B16 = jnp.float32, jnp.bfloat16
 NT = (((1,), (1,)), ((), ()))
 TN = (((0,), (0,)), ((), ()))
@@ -156,7 +156,7 @@
     def pass_on(src, k, s):
         slot = lax.rem(k, SLOTS)
         for way in range(2):
-            @pl.when(sends(way))
+            @pl.when(sends(way) & (s < nb - way))
             def _():
                 @pl.when((s == first_block(k, c)) & (k >= SLOTS))
                 def _():
@@ -269,7 +269,7 @@
 
             @pl.when(k >= SLOTS)
             def _():
-                pl.semaphore_wait(row_free, GRID - 1)
+                pl.semaphore_wait(row_free.at[lax.rem(lax.div(k, GRID), SLOTS // GRID)], GRID - 1)
 
         early = (r == lax.rem(k + 1, GRID)) & (k + 1 < steps)
 
@@ -308,6 +308,8 @@
         def _():
             pl.semaphore_signal(inv_free.at[lax.rem(r - c + GRID, GRID) - 1], inc=1, device_id={"row": lax.rem(k, GRID)}, device_id_type=MESH)
 
+    top = nb - jnp.where(r < c, 1, 0)
+
     def columns(k, lo, hi):
         def column(s):
             first = jnp.maximum(first_block(k, r), s)
@@ -333,7 +335,7 @@
         def _():
             loop(first_block(k, r), nb, lambda t: take_row(k, t))
 
-        columns(k, s_lo, jnp.where(soon, s_lo + 1, nb))
+        columns(k, s_lo, jnp.where(soon, jnp.minimum(s_lo + 1, top), top))
 
     def finish(k):
         d = lax.rem(k, GRID)
@@ -355,14 +357,14 @@
         for way in range(2):
             @pl.when(sends(way))
             def _():
-                loop(first_block(k, c), nb, lambda s: chain_copy(col_pan, lax.rem(k, SLOTS), s, way).wait_send())
+                loop(first_block(k, c), nb - way, lambda s: chain_copy(col_pan, lax.rem(k, SLOTS), s, way).wait_send())
 
         @pl.when((c != d) & (k + SLOTS < last + r))
         def _():
-            pl.semaphore_signal(row_free, inc=1, device_id={"col": d}, device_id_type=MESH)
+            pl.semaphore_signal(row_free.at[lax.rem(lax.div(k, GRID), SLOTS // GRID)], inc=1, device_id={"col": d}, device_id_type=MESH)
 
         for way in range(2):
-            @pl.when((k + SLOTS < last + c) & ((r > c) if way == 0 else (r < c)))
+            @pl.when((k + SLOTS < last - way * GRID + c) & ((r > c) if way == 0 else (r < c)))
             def _():
                 pl.semaphore_signal(chain_free.at[way], inc=1, device_id={"row": r - 1 + 2 * way}, device_id_type=MESH)
 
@@ -388,7 +390,9 @@
 
         @pl.when(r != c)
         def _():
-            take_col(k, s1)
+            @pl.when(s1 < top)
+            def _():
+                take_col(k, s1)
 
             t = first_block(k, r)
 
@@ -416,7 +420,7 @@
 
             @pl.when(k > 1)
             def _():
-                columns(k - 2, lax.div(k, GRID) + 1, nb)
+                columns(k - 2, lax.div(k, GRID) + 1, top)
 
         @pl.when(k == 1)
         def _():
@@ -479,7 +483,7 @@
                 dma((3,)),
                 dma,
                 dma,
-                reg,
+                reg((SLOTS // GRID,)),
                 reg((GRID - 1,)),
                 reg((2,)),
                 reg,

time: 583 us -> 555 us (0.952)
  Pallas kernels: 567 us -> 543 us
    pallas_call x1, Pallas kernels: 567 us -> 543 us  [factor_local(): pl.pallas_call(functools.partial(kernel, nb), out_shape=jax.ShapeDtypeStr...]
where the time goes in v4:
time: 555 us
  Pallas kernels  543 us (98%)
  other arithmetic  12.3 us (2%)
    pallas_call x1, Pallas kernels, factor_local(): pl.pallas_call(functools.partial(kernel, nb), out_shape=jax.ShapeDtypeStr...  543 us
    select_n x1, other arithmetic, factor_local(): jnp.where(keep, work.reshape(nb, blk, width // blk, blk), 0.0)  12.3 us

profile of v4, /device:TPU:31, one launch (start us, length us, event | category | flops | bytes accessed | tf_op | source)
XLA Modules:
  0.0 555.1 jit_solution(8037137270932340239)
XLA Ops:
  0.0 0.1 broadcast_compare_fusion
  0.1 0.1 broadcast_in_dim.18
  0.2 542.7 %shard_map.17 = f32[8,256,2048]{2,1,0:T(8,128)} custom-call(f32[8,256,2048]{2,1,0:T(8,128)} %a_ref.1), custom_call_target="tpu_custom_call" | custom-call | tf_op jit(solution)/shard_map/pallas_call | solution.py:461
  542.8 12.3 %broadcast_select_fusion = f32[8,256,2048]{2,1,0:T(8,128)} fusion(f32[8,256,2048]{2,1,0:T(8,128)} %shard_map.17, pred[8,2048]{1,0:T(8,128)(4,1)S(1)} %bitcast.1), kind=kLoop, calls=%fused_computation | loop fusion | flops 4194304 | bytes 33570816 | tf_op jit(solution)/shard_map/jit(_where)/select_n | solution.py:499
  (1 shorter events, 0.0 us)

commit v5 on v4

--- a/solution.py
+++ b/solution.py
@@ -65,8 +65,8 @@
     return jnp.concatenate(done, axis=0)
 
 
-def kernel(nb, a_ref, o_ref, mat, row_pan, col_pan, inv_a, inv_b, nxt_a, nxt_b, nxt_x, load_sem, br_recv, bc_recv,
-           row_send, relay_send, chain_send, inv_recv, inv_send, nxt_recv, x_recv, x_send, row_free, inv_free, chain_free, nxt_free, x_free):
+def kernel(nb, a_ref, o_ref, mat, row_pan, col_pan, inv_a, inv_b, nxt_a, nxt_b, nxt_x, nxt_y, x_out, load_sem, br_recv, bc_recv,
+           row_send, relay_send, chain_send, inv_recv, inv_send, nxt_recv, x_recv, x_send, y_recv, y_send, row_free, inv_free, chain_free, nxt_free, x_free):
     r = lax.axis_index("row")
     c = lax.axis_index("col")
     steps = nb * GRID
@@ -143,9 +143,17 @@
 
     def x_copy(k):
         return pltpu.make_async_remote_copy(
-            src_ref=mat.at[lax.div(k, GRID), rows_of(lax.div(k + 1, GRID)), :], dst_ref=nxt_x,
-            send_sem=x_send, recv_sem=x_recv,
+            src_ref=x_out, dst_ref=nxt_x, send_sem=x_send, recv_sem=x_recv,
             device_id={"col": lax.rem(c + 1, GRID)}, device_id_type=MESH)
+
+    def x_stage(k):
+        x_out[...] = mat[lax.div(k, GRID), rows_of(lax.div(k + 1, GRID)), :]
+
+    def y_copy(k):
+        return pltpu.make_async_remote_copy(
+            src_ref=row_pan.at[lax.rem(k, SLOTS), rows_of(lax.div(k + 1, GRID)), :], dst_ref=nxt_y,
+            send_sem=y_send, recv_sem=y_recv,
+            device_id={"row": lax.rem(r + 1, GRID), "col": lax.rem(c + 1, GRID)}, device_id_type=MESH)
 
     def gather_inv(a, b):
         return jnp.concatenate([jnp.concatenate([a[...], jnp.zeros((HALF, HALF), F32)], axis=1), b[...]], axis=0)
@@ -209,10 +217,6 @@
         @pl.when(k >= GRID)
         def _():
             for_peers(lambda off: pl.semaphore_wait(inv_free.at[off - 1], 1))
-
-            @pl.when(k + 1 < steps)
-            def _():
-                pl.semaphore_wait(nxt_free, 1)
 
         def send(part):
             @pl.when(k + 1 < steps)
@@ -304,6 +308,10 @@
             for part in range(3):
                 nxt_copy(part).wait_send()
 
+            @pl.when(k > 0)
+            def _():
+                y_copy(k - 1).wait_send()
+
         @pl.when((r != c) & (k + GRID < last + r))
         def _():
             pl.semaphore_signal(inv_free.at[lax.rem(r - c + GRID, GRID) - 1], inc=1, device_id={"row": lax.rem(k, GRID)}, device_id_type=MESH)
@@ -375,12 +383,25 @@
         def _():
             slot = lax.rem(k, SLOTS)
             x_copy(k).wait_recv()
+
+            @pl.when(k > 0)
+            def _():
+                y_copy(k - 1).wait_recv()
+                prod = lax.dot_general(row_pan[lax.rem(k - 1 + SLOTS, SLOTS), rows_of(s1), :], nxt_y[...], NT, preferred_element_type=F32)
+                nxt_x[...] = nxt_x[...] - prod
             for part in range(3):
                 nxt_copy(part).wait_recv()
             sol = lax.dot_general(nxt_x[...], gather_inv(nxt_a, nxt_b), NT, precision=HIGH, preferred_element_type=F32).astype(B16)
             row_pan[slot, rows_of(s1), :] = sol
             col_pan[slot, rows_of(s1), :] = sol
             mat[s1, rows_of(s1), :] = mat[s1, rows_of(s1), :] - lax.dot_general(sol, sol, NT, preferred_element_type=F32)
+
+            @pl.when(k + 2 < steps)
+            def _():
+                @pl.when(k + 1 >= GRID)
+                def _():
+                    pl.semaphore_wait(nxt_free, 1)
+                y_copy(k).start()
             pass_on(row_pan, k, s1)
 
             @pl.when(k + GRID + 1 < steps)
@@ -400,13 +421,6 @@
             def _():
                 take_row(k, t)
                 update(k, t, s1, 1)
-
-                @pl.when((r == lax.rem(k + 2, GRID)) & (k + 2 < steps))
-                def _():
-                    @pl.when(k + 1 >= GRID)
-                    def _():
-                        pl.semaphore_wait(x_free, 1)
-                    x_copy(k + 1).start()
 
     def step(k):
         d = lax.rem(k, GRID)
@@ -432,9 +446,22 @@
         def _():
             trail(k - 1)
 
+        ready = (c == lax.rem(k + 1, GRID)) & (r == lax.rem(k + 2, GRID)) & (k + 2 < steps)
+
+        @pl.when(ready)
+        def _():
+            x_stage(k + 1)
+
         @pl.when(k > 1)
         def _():
             finish(k - 2)
+
+        @pl.when(ready)
+        def _():
+            @pl.when(k + 1 >= GRID)
+            def _():
+                pl.semaphore_wait(x_free, 1)
+            x_copy(k + 1).start()
 
         @pl.when((c == lax.rem(k + 1, GRID)) & (k + 1 < steps))
         def _():
@@ -442,6 +469,7 @@
 
     @pl.when((r == 1) & (c == 0))
     def _():
+        x_stage(0)
         x_copy(0).start()
 
     loop(0, steps, step)
@@ -472,6 +500,8 @@
                 pltpu.VMEM((HALF, HALF), F32),
                 pltpu.VMEM((HALF, BLK), F32),
                 pltpu.VMEM((BLK, BLK), F32),
+                pltpu.VMEM((BLK, BLK), B16),
+                pltpu.VMEM((BLK, BLK), F32),
                 dma((nb, nb)),
                 dma((SLOTS, nb)),
                 dma((SLOTS, nb)),
@@ -483,13 +513,15 @@
                 dma((3,)),
                 dma,
                 dma,
+                dma,
+                dma,
                 reg((SLOTS // GRID,)),
                 reg((GRID - 1,)),
                 reg((2,)),
                 reg,
                 reg,
             ],
-            compiler_params=pltpu.CompilerParams(collective_id=0, has_side_effects=True, vmem_limit_bytes=56 * 1024 * 1024),
+            compiler_params=pltpu.CompilerParams(collective_id=0, has_side_effects=True, vmem_limit_bytes=36 * 1024 * 1024),
         )(a_loc)
         row_id = lax.axis_index("row")
         col_id = lax.axis_index("col")

time: 555 us -> 531 us (0.957)
  Pallas kernels: 543 us -> 523 us
    pallas_call x1, Pallas kernels: 543 us -> 523 us  [factor_local(): pl.pallas_call(functools.partial(kernel, nb), out_shape=jax.ShapeDtypeStr...]
where the time goes in v5:
time: 531 us
  Pallas kernels  523 us (98%)
  other arithmetic  7.68 us (1%)
    pallas_call x1, Pallas kernels, factor_local(): pl.pallas_call(functools.partial(kernel, nb), out_shape=jax.ShapeDtypeStr...  523 us

profile of v5, /device:TPU:31, one launch (start us, length us, event | category | flops | bytes accessed | tf_op | source)
XLA Modules:
  0.0 530.6 jit_solution(16568492254325202336)
XLA Ops:
  0.0 0.1 broadcast_compare_fusion
  0.1 0.1 broadcast_in_dim.18
  0.2 522.8 %shard_map.17 = f32[8,256,2048]{2,1,0:T(8,128)S(1)} custom-call(f32[8,256,2048]{2,1,0:T(8,128)} %a_ref.1), custom_call_target="tpu_custom_call" | custom-call | tf_op jit(solution)/shard_map/pallas_call | solution.py:489
  523.0 7.6 %broadcast_select_fusion = f32[8,256,2048]{2,1,0:T(8,128)} fusion(f32[8,256,2048]{2,1,0:T(8,128)S(1)} %shard_map.17, pred[8,2048]{1,0:T(8,128)(4,1)S(1)} %bitcast.1), kind=kLoop, calls=%fused_computation | loop fusion | flops 4194304 | bytes 33570816 | tf_op jit(solution)/shard_map/jit(_where)/select_n | solution.py:531
  (1 shorter events, 0.0 us)

commit v6 on v5

--- a/solution.py
+++ b/solution.py
@@ -65,12 +65,25 @@
     return jnp.concatenate(done, axis=0)
 
 
-def kernel(nb, a_ref, o_ref, mat, row_pan, col_pan, inv_a, inv_b, nxt_a, nxt_b, nxt_x, nxt_y, x_out, load_sem, br_recv, bc_recv,
-           row_send, relay_send, chain_send, inv_recv, inv_send, nxt_recv, x_recv, x_send, y_recv, y_send, row_free, inv_free, chain_free, nxt_free, x_free):
+def far_reach(nb):
+    return 21 * nb // 8
+
+
+def hist_at(t, nb):
+    base = (far_reach(nb) + 1) // GRID
+    m = t - base
+    return m * (GRID * (base + 1) - 1 - far_reach(nb)) + m * (m - 1) * (GRID // 2)
+
+
+def kernel(nb, a_ref, o_ref, mat, row_pan, col_pan, inv_a, inv_b, nxt_a, nxt_b, nxt_x, nxt_y, x_out, hist, far_col, load_sem, br_recv, bc_recv,
+           row_send, relay_send, chain_send, inv_recv, inv_send, nxt_recv, x_recv, x_send, y_recv, y_send, row_free, inv_free, chain_free, nxt_free, x_free, far_recv, far_send,
+           far_free):
     r = lax.axis_index("row")
     c = lax.axis_index("col")
     steps = nb * GRID
     last = GRID * (nb - 1)
+    reach = far_reach(nb)
+    base = (reach + 1) // GRID
 
     def first_block(k, pos):
         return lax.div(k + GRID - pos, GRID)
@@ -161,10 +174,13 @@
     def sends(way):
         return ((r >= c) & (r < GRID - 1)) if way == 0 else ((r <= c) & (r > 0))
 
+    def near(k):
+        return jnp.minimum(nb, lax.div(k + reach - c, GRID) + 1)
+
     def pass_on(src, k, s):
         slot = lax.rem(k, SLOTS)
         for way in range(2):
-            @pl.when(sends(way) & (s < nb - way))
+            @pl.when(sends(way) & (s < jnp.minimum(near(k), nb - way)))
             def _():
                 @pl.when((s == first_block(k, c)) & (k >= SLOTS))
                 def _():
@@ -343,7 +359,70 @@
         def _():
             loop(first_block(k, r), nb, lambda t: take_row(k, t))
 
-        columns(k, s_lo, jnp.where(soon, jnp.minimum(s_lo + 1, top), top))
+        @pl.when(k < steps - 1 - reach)
+        def _():
+            for t in range(base, nb):
+                @pl.when(k < GRID * t + GRID - 1 - reach)
+                def _():
+                    hist[hist_at(t, nb) + k] = row_pan[lax.rem(k, SLOTS), t * BLK : (t + 1) * BLK, :]
+
+        hi = jnp.minimum(top, near(k))
+        columns(k, s_lo, jnp.where(soon, jnp.minimum(s_lo + 1, hi), hi))
+
+    def far_copy(src, kp, way):
+        return pltpu.make_async_remote_copy(
+            src_ref=src, dst_ref=far_col.at[kp], send_sem=far_send.at[kp, way], recv_sem=far_recv.at[kp],
+            device_id={"row": r + 1 - 2 * way}, device_id_type=MESH)
+
+    def far_sent(j, way):
+        return (j > reach) & (j < steps) & (lax.div(j, GRID) < nb - way)
+
+    def far_pass(src, j, kp):
+        for way in range(2):
+            @pl.when(sends(way) & far_sent(j, way))
+            def _():
+                @pl.when((kp == 0) & (j - GRID > reach))
+                def _():
+                    pl.semaphore_wait(far_free.at[way], 1)
+                far_copy(src, kp, way).start()
+
+    def far_start(j):
+        @pl.when((r == c) & (c == lax.rem(j, GRID)) & (j > reach) & (j < steps))
+        def _():
+            loop(0, j - reach, lambda kp: far_pass(hist.at[hist_at(lax.div(j, GRID), nb) + kp], j, kp))
+
+    def far_take(j):
+        s = lax.div(j, GRID)
+
+        @pl.when((c == lax.rem(j, GRID)) & (j > reach) & (j < steps) & (s < top))
+        def _():
+            def one(kp):
+                @pl.when(r == c)
+                def _():
+                    far_col[kp] = hist[hist_at(s, nb) + kp]
+
+                @pl.when(r != c)
+                def _():
+                    far_copy(far_col.at[kp], kp, 0).wait_recv()
+                    far_pass(far_col.at[kp], j, kp)
+
+                def tile(t):
+                    prod = lax.dot_general(hist[hist_at(t, nb) + kp], far_col[kp], NT, preferred_element_type=F32)
+                    mat[s, rows_of(t), :] = mat[s, rows_of(t), :] - prod
+                loop(s + jnp.where(r < c, 1, 0), nb, tile)
+            loop(0, j - reach, one)
+
+    def far_done(j):
+        @pl.when((c == lax.rem(j, GRID)) & (j > reach) & (j < steps))
+        def _():
+            for way in range(2):
+                @pl.when(sends(way) & far_sent(j, way))
+                def _():
+                    loop(0, j - reach, lambda kp: far_copy(far_col.at[kp], kp, way).wait_send())
+
+                @pl.when(far_sent(j + GRID, way) & ((r > c) if way == 0 else (r < c)))
+                def _():
+                    pl.semaphore_signal(far_free.at[way], inc=1, device_id={"row": r - 1 + 2 * way}, device_id_type=MESH)
 
     def finish(k):
         d = lax.rem(k, GRID)
@@ -365,7 +444,7 @@
         for way in range(2):
             @pl.when(sends(way))
             def _():
-                loop(first_block(k, c), nb - way, lambda s: chain_copy(col_pan, lax.rem(k, SLOTS), s, way).wait_send())
+                loop(first_block(k, c), jnp.minimum(near(k), nb - way), lambda s: chain_copy(col_pan, lax.rem(k, SLOTS), s, way).wait_send())
 
         @pl.when((c != d) & (k + SLOTS < last + r))
         def _():
@@ -434,7 +513,7 @@
 
             @pl.when(k > 1)
             def _():
-                columns(k - 2, lax.div(k, GRID) + 1, top)
+                columns(k - 2, lax.div(k, GRID) + 1, jnp.minimum(top, near(k - 2)))
 
         @pl.when(k == 1)
         def _():
@@ -442,9 +521,14 @@
                 for t in range(nb):
                     load(t, s).wait()
 
+        far_done(k - 1)
+        far_take(k + 2)
+
         @pl.when(k > 0)
         def _():
             trail(k - 1)
+
+        far_start(k + 3)
 
         ready = (c == lax.rem(k + 1, GRID)) & (r == lax.rem(k + 2, GRID)) & (k + 2 < steps)
 
@@ -473,6 +557,7 @@
         x_copy(0).start()
 
     loop(0, steps, step)
+    far_done(steps - 1)
     finish(steps - 2)
     finish(steps - 1)
 
@@ -484,6 +569,7 @@
 def solution(mesh):
     def factor_local(a_loc):
         nb, blk, width = a_loc.shape
+        far = nb * GRID - 1 - far_reach(nb)
         dma = pltpu.SemaphoreType.DMA
         reg = pltpu.SemaphoreType.REGULAR
         work = pl.pallas_call(
@@ -502,6 +588,8 @@
                 pltpu.VMEM((BLK, BLK), F32),
                 pltpu.VMEM((BLK, BLK), B16),
                 pltpu.VMEM((BLK, BLK), F32),
+                pltpu.VMEM((hist_at(nb, nb), blk, blk), B16),
+                pltpu.VMEM((far, blk, blk), B16),
                 dma((nb, nb)),
                 dma((SLOTS, nb)),
                 dma((SLOTS, nb)),
@@ -520,8 +608,11 @@
                 reg((2,)),
                 reg,
                 reg,
+                dma((far,)),
+                dma((far, 2)),
+                reg((2,)),
             ],
-            compiler_params=pltpu.CompilerParams(collective_id=0, has_side_effects=True, vmem_limit_bytes=36 * 1024 * 1024),
+            compiler_params=pltpu.CompilerParams(collective_id=0, has_side_effects=True, vmem_limit_bytes=75 * 512 * 1024),
         )(a_loc)
         row_id = lax.axis_index("row")
         col_id = lax.axis_index("col")

time: 531 us -> 518 us (0.976)
  Pallas kernels: 523 us -> 510 us
    pallas_call x1, Pallas kernels: 523 us -> 510 us  [factor_local(): pl.pallas_call(functools.partial(kernel, nb), out_shape=jax.ShapeDtypeStr...]
where the time goes in v6:
time: 518 us; the launch traced here: 517 us
  Pallas kernels  510 us (98%)
  other arithmetic  7.68 us (1%)
    pallas_call x1, Pallas kernels, factor_local(): pl.pallas_call(functools.partial(kernel, nb), out_shape=jax.ShapeDtypeStr...  510 us

profile of v6, /device:TPU:31, one launch (start us, length us, event | category | flops | bytes accessed | tf_op | source)
XLA Modules:
  0.0 517.5 jit_solution(11086259316456378638)
XLA Ops:
  0.0 0.1 broadcast_compare_fusion
  0.1 0.1 broadcast_in_dim.18
  0.2 509.7 %shard_map.17 = f32[8,256,2048]{2,1,0:T(8,128)S(1)} custom-call(f32[8,256,2048]{2,1,0:T(8,128)} %a_ref.1), custom_call_target="tpu_custom_call" | custom-call | tf_op jit(solution)/shard_map/pallas_call | solution.py:575
  509.9 7.6 %broadcast_select_fusion = f32[8,256,2048]{2,1,0:T(8,128)} fusion(f32[8,256,2048]{2,1,0:T(8,128)S(1)} %shard_map.17, pred[8,2048]{1,0:T(8,128)(4,1)S(1)} %bitcast.1), kind=kLoop, calls=%fused_computation | loop fusion | flops 4194304 | bytes 33570816 | tf_op jit(solution)/shard_map/jit(_where)/select_n | solution.py:622
  (1 shorter events, 0.0 us)

commit v7 on v6

--- a/solution.py
+++ b/solution.py
@@ -14,6 +14,7 @@
 HALF = 128
 PAN = 16
 SLOTS = 8
+VIA = 1
 F32, B16 = jnp.float32, jnp.bfloat16
 NT = (((1,), (1,)), ((), ()))
 TN = (((0,), (0,)), ((), ()))
@@ -76,7 +77,7 @@
 
 
 def kernel(nb, a_ref, o_ref, mat, row_pan, col_pan, inv_a, inv_b, nxt_a, nxt_b, nxt_x, nxt_y, x_out, hist, far_col, load_sem, br_recv, bc_recv,
-           row_send, relay_send, chain_send, inv_recv, inv_send, nxt_recv, x_recv, x_send, y_recv, y_send, row_free, inv_free, chain_free, nxt_free, x_free, far_recv, far_send,
+           row_send, relay_send, chain_send, inv_recv, inv_send, nxt_recv, x_recv, x_send, y_recv, y_send, row_free, inv_free, chain_free, nxt_free, x_free, via_free, far_recv, far_send,
            far_free):
     r = lax.axis_index("row")
     c = lax.axis_index("col")
@@ -152,7 +153,17 @@
         return pltpu.make_async_remote_copy(
             src_ref=inv_part(inv_a, inv_b, part), dst_ref=inv_part(nxt_a, nxt_b, part),
             send_sem=inv_send.at[0, part], recv_sem=nxt_recv.at[part],
-            device_id={"row": lax.rem(r + 1, GRID), "col": lax.rem(c + 1, GRID)}, device_id_type=MESH)
+            device_id={"row": jnp.where(r == VIA, r, lax.rem(r + 1, GRID)), "col": lax.rem(c + 1, GRID)}, device_id_type=MESH)
+
+    def via_copy(part):
+        ref = inv_part(nxt_a, nxt_b, part) if part < 3 else nxt_y
+        return pltpu.make_async_remote_copy(
+            src_ref=ref, dst_ref=ref, send_sem=inv_send.at[0, part] if part < 3 else y_send,
+            recv_sem=nxt_recv.at[part] if part < 3 else y_recv,
+            device_id={"row": lax.rem(r + 1, GRID)}, device_id_type=MESH)
+
+    def via(k):
+        return (lax.rem(k, GRID) == VIA) & (r == VIA) & (c == VIA + 1) & (k + 1 < steps)
 
     def x_copy(k):
         return pltpu.make_async_remote_copy(
@@ -166,7 +177,7 @@
         return pltpu.make_async_remote_copy(
             src_ref=row_pan.at[lax.rem(k, SLOTS), rows_of(lax.div(k + 1, GRID)), :], dst_ref=nxt_y,
             send_sem=y_send, recv_sem=y_recv,
-            device_id={"row": lax.rem(r + 1, GRID), "col": lax.rem(c + 1, GRID)}, device_id_type=MESH)
+            device_id={"row": jnp.where(r == VIA, r, lax.rem(r + 1, GRID)), "col": lax.rem(c + 1, GRID)}, device_id_type=MESH)
 
     def gather_inv(a, b):
         return jnp.concatenate([jnp.concatenate([a[...], jnp.zeros((HALF, HALF), F32)], axis=1), b[...]], axis=0)
@@ -480,6 +491,10 @@
                 @pl.when(k + 1 >= GRID)
                 def _():
                     pl.semaphore_wait(nxt_free, 1)
+
+                @pl.when((k + 1 >= GRID + VIA) & (r == VIA))
+                def _():
+                    pl.semaphore_wait(via_free, 1)
                 y_copy(k).start()
             pass_on(row_pan, k, s1)
 
@@ -521,6 +536,12 @@
                 for t in range(nb):
                     load(t, s).wait()
 
+        @pl.when(via(k))
+        def _():
+            for part in (3, 0, 1, 2):
+                via_copy(part).wait_recv()
+                via_copy(part).start()
+
         far_done(k - 1)
         far_take(k + 2)
 
@@ -550,6 +571,15 @@
         @pl.when((c == lax.rem(k + 1, GRID)) & (k + 1 < steps))
         def _():
             ahead(k)
+
+        @pl.when(via(k))
+        def _():
+            for part in range(4):
+                via_copy(part).wait_send()
+
+            @pl.when(k + GRID + 1 < steps)
+            def _():
+                pl.semaphore_signal(via_free, inc=1, device_id={"col": VIA}, device_id_type=MESH)
 
     @pl.when((r == 1) & (c == 0))
     def _():
@@ -608,6 +638,7 @@
                 reg((2,)),
                 reg,
                 reg,
+                reg,
                 dma((far,)),
                 dma((far, 2)),
                 reg((2,)),

time: 518 us -> 495 us (0.956)
  Pallas kernels: 510 us -> 488 us
    pallas_call x1, Pallas kernels: 510 us -> 488 us  [factor_local(): pl.pallas_call(functools.partial(kernel, nb), out_shape=jax.ShapeDtypeStr...]
where the time goes in v7:
time: 495 us
  Pallas kernels  488 us (99%)
  other arithmetic  7.68 us (2%)
    pallas_call x1, Pallas kernels, factor_local(): pl.pallas_call(functools.partial(kernel, nb), out_shape=jax.ShapeDtypeStr...  488 us

profile of v7, /device:TPU:31, one launch (start us, length us, event | category | flops | bytes accessed | tf_op | source)
XLA Modules:
  0.0 495.4 jit_solution(2363707769812348202)
XLA Ops:
  0.0 0.1 broadcast_compare_fusion
  0.1 0.1 broadcast_in_dim.18
  0.2 487.6 %shard_map.17 = f32[8,256,2048]{2,1,0:T(8,128)S(1)} custom-call(f32[8,256,2048]{2,1,0:T(8,128)} %a_ref.1), custom_call_target="tpu_custom_call" | custom-call | tf_op jit(solution)/shard_map/pallas_call | solution.py:605
  487.7 7.6 %broadcast_select_fusion = f32[8,256,2048]{2,1,0:T(8,128)} fusion(f32[8,256,2048]{2,1,0:T(8,128)S(1)} %shard_map.17, pred[8,2048]{1,0:T(8,128)(4,1)S(1)} %bitcast.1), kind=kLoop, calls=%fused_computation | loop fusion | flops 4194304 | bytes 33570816 | tf_op jit(solution)/shard_map/jit(_where)/select_n | solution.py:653
  (1 shorter events, 0.0 us)

commit v8 on v7

--- a/solution.py
+++ b/solution.py
@@ -155,6 +155,15 @@
             send_sem=inv_send.at[0, part], recv_sem=nxt_recv.at[part],
             device_id={"row": jnp.where(r == VIA, r, lax.rem(r + 1, GRID)), "col": lax.rem(c + 1, GRID)}, device_id_type=MESH)
 
+    def hand_copy(part):
+        return pltpu.make_async_remote_copy(
+            src_ref=inv_part(inv_a, inv_b, part), dst_ref=inv_part(nxt_a, nxt_b, part),
+            send_sem=inv_send.at[0, part], recv_sem=nxt_recv.at[part],
+            device_id={"col": lax.rem(c + 1, GRID)}, device_id_type=MESH)
+
+    def hands(k):
+        return (lax.rem(k, 2) == 0) & (r == lax.rem(k + 1, GRID))
+
     def via_copy(part):
         ref = inv_part(nxt_a, nxt_b, part) if part < 3 else nxt_y
         return pltpu.make_async_remote_copy(
@@ -246,7 +255,7 @@
             for_peers(lambda off: pl.semaphore_wait(inv_free.at[off - 1], 1))
 
         def send(part):
-            @pl.when(k + 1 < steps)
+            @pl.when((k + 1 < steps) & (lax.rem(k, 2) == 1))
             def _():
                 nxt_copy(part).start()
             inv_ways(k, lambda way: inv_copy(way, part).start())
@@ -296,6 +305,10 @@
             def _():
                 for part in range(3):
                     inv_copy(0, part).wait_recv()
+
+                    @pl.when(hands(k))
+                    def _():
+                        hand_copy(part).start()
                     inv_ways(k, lambda way: inv_copy(way, part).start())
 
             @pl.when(k >= SLOTS)
@@ -330,10 +343,17 @@
             for part in range(3):
                 inv_ways(k, lambda way: inv_copy(way, part).wait_send())
 
+        @pl.when((k < last + r) & hands(k))
+        def _():
+            for part in range(3):
+                hand_copy(part).wait_send()
+
         @pl.when((r == c) & (k + 1 < steps))
         def _():
-            for part in range(3):
-                nxt_copy(part).wait_send()
+            @pl.when(lax.rem(k, 2) == 1)
+            def _():
+                for part in range(3):
+                    nxt_copy(part).wait_send()
 
             @pl.when(k > 0)
             def _():

time: 495 us -> 490 us (0.990)
  Pallas kernels: 488 us -> 482 us
    pallas_call x1, Pallas kernels: 488 us -> 482 us  [factor_local(): pl.pallas_call(functools.partial(kernel, nb), out_shape=jax.ShapeDtypeStr...]
where the time goes in v8:
time: 490 us
  Pallas kernels  482 us (98%)
  other arithmetic  7.68 us (2%)
    pallas_call x1, Pallas kernels, factor_local(): pl.pallas_call(functools.partial(kernel, nb), out_shape=jax.ShapeDtypeStr...  482 us

profile of v8, /device:TPU:31, one launch (start us, length us, event | category | flops | bytes accessed | tf_op | source)
XLA Modules:
  0.0 489.9 jit_solution(9144668235140915805)
XLA Ops:
  0.0 0.1 broadcast_compare_fusion
  0.1 0.1 broadcast_in_dim.18
  0.2 482.1 %shard_map.17 = f32[8,256,2048]{2,1,0:T(8,128)S(1)} custom-call(f32[8,256,2048]{2,1,0:T(8,128)} %a_ref.1), custom_call_target="tpu_custom_call" | custom-call | tf_op jit(solution)/shard_map/pallas_call | solution.py:625
  482.3 7.6 %broadcast_select_fusion = f32[8,256,2048]{2,1,0:T(8,128)} fusion(f32[8,256,2048]{2,1,0:T(8,128)S(1)} %shard_map.17, pred[8,2048]{1,0:T(8,128)(4,1)S(1)} %bitcast.1), kind=kLoop, calls=%fused_computation | loop fusion | flops 4194304 | bytes 33570816 | tf_op jit(solution)/shard_map/jit(_where)/select_n | solution.py:673
  (1 shorter events, 0.0 us)
